TPU v7x, 32 devices: a whole 2x2x4 slice. The times are simulated.
32 devices in a mesh: row: 4 (over y, x), col: 4 (over z), crop: 2 (over core).
Axes of the slice: x: 2, y: 2, z: 4, core: 2. Of those that a mesh axis runs over, the one named last changes fastest.
Arguments:
- pair_repr: bfloat16 [256, 128, 128], P(('crop', 'row'), 'col'), parts along dimension 0, may hold values from -6 to 6
- pair_mask: int32 [256, 128], P(('crop', 'row'), 'col'), parts along dimension 0, may hold values 0 or 1
- out_left_w: bfloat16 [128, 256], replicated, may hold values from -0.5 to 0.5
- out_right_w: bfloat16 [128, 256], replicated, may hold values from -0.5 to 0.5
- out_gate_w: bfloat16 [128, 128], replicated, may hold values from -0.5 to 0.5
- out_final_w: bfloat16 [128, 128], replicated, may hold values from -0.5 to 0.5
- in_left_w: bfloat16 [128, 256], replicated, may hold values from -0.5 to 0.5
- in_right_w: bfloat16 [128, 256], replicated, may hold values from -0.5 to 0.5
- in_gate_w: bfloat16 [128, 128], replicated, may hold values from -0.5 to 0.5
- in_final_w: bfloat16 [128, 128], replicated, may hold values from -0.5 to 0.5
- trans_in_w: bfloat16 [128, 1024], replicated, may hold values from -0.5 to 0.5
- trans_out_w: bfloat16 [512, 128], replicated, may hold values from -0.25 to 0.25
Outputs:
- pair_out: bfloat16 [256, 128, 128], P(('crop', 'row'), 'col'), parts along dimension 0
There are 2 independent parts, one for each index of `crop`. A program takes and returns all parts, laid end to end along the dimension named above; an argument that names none is the same for every part. Nothing has to cross between parts.
All inputs are finite; a program needn't handle non-finite values. No bound on the sum of `pair_mask` on one device may be relied on, other than what follows from the above.
Results may differ from a plain program's by a relative error of at most 0.015.
Values may be sent and summed in bfloat16 or wider, within the bound.
No kernel may reach another device: no remote copies, remote signals or barrier semaphores. Data moves between devices by JAX's collectives and lax.ppermute only.
A program may use at most 128 MiB of HBM per device.

v0:
```python
import jax
import jax.numpy as jnp
from jax import lax
from jax.sharding import PartitionSpec as P

epsilon = 1e-05


def layer_norm(values):
    average = jnp.mean(values, axis=-1, keepdims=True)
    centered = values - average
    spread = jnp.mean(centered * centered, axis=-1, keepdims=True)
    return centered * lax.rsqrt(spread + epsilon)


def gated(normed, weight, mask_vals):
    projected = jnp.dot(normed, weight, preferred_element_type=jnp.float32)
    half_width = weight.shape[1] // 2
    result = jax.nn.sigmoid(projected[..., :half_width]) * projected[..., half_width:]
    result = result * mask_vals[..., None]
    return result.astype(jnp.bfloat16)


def finish(pair_repr, normed, triangle, gate_w, final_w):
    gate_vals = jax.nn.sigmoid(jnp.dot(normed, gate_w, preferred_element_type=jnp.float32))
    tri_norm = layer_norm(triangle).astype(jnp.bfloat16)
    update = jnp.dot(tri_norm, final_w, preferred_element_type=jnp.float32)
    return (pair_repr.astype(jnp.float32) + gate_vals * update).astype(jnp.bfloat16)


def shards(
    pair_repr,
    pair_mask,
    out_left_w,
    out_right_w,
    out_gate_w,
    out_final_w,
    in_left_w,
    in_right_w,
    in_gate_w,
    in_final_w,
    trans_in_w,
    trans_out_w,
):
    mask_vals = pair_mask.astype(jnp.float32)
    normed_out = layer_norm(pair_repr.astype(jnp.float32)).astype(jnp.bfloat16)
    outbound = gated(normed_out, out_right_w, mask_vals)
    turned_right = lax.all_to_all(
        lax.all_to_all(outbound, "row", split_axis=0, concat_axis=0, tiled=True),
        "col",
        split_axis=0,
        concat_axis=1,
        tiled=True,
    )
    left_tile = gated(normed_out, out_left_w, mask_vals)
    gathered = lax.all_gather(left_tile, "col", axis=1, tiled=True)
    triangle = jnp.einsum(
        "ikh,jkh->ijh",
        gathered,
        lax.all_gather(turned_right, "row", axis=0, tiled=True),
        preferred_element_type=jnp.float32,
    )
    middle = finish(pair_repr, normed_out, triangle, out_gate_w, out_final_w)
    normed_in = layer_norm(middle.astype(jnp.float32)).astype(jnp.bfloat16)
    outbound_left = gated(normed_in, in_left_w, mask_vals)
    turned_left = lax.all_to_all(
        lax.all_to_all(outbound_left, "col", split_axis=1, concat_axis=1, tiled=True),
        "row",
        split_axis=1,
        concat_axis=0,
        tiled=True,
    )
    right_tile = gated(normed_in, in_right_w, mask_vals)
    column_panel = lax.all_gather(right_tile, "row", axis=0, tiled=True)
    triangle_in = jnp.einsum(
        "kih,kjh->ijh",
        lax.all_gather(turned_left, "col", axis=1, tiled=True),
        column_panel,
        preferred_element_type=jnp.float32,
    )
    after_in = finish(middle, normed_in, triangle_in, in_gate_w, in_final_w)
    normed_mix = layer_norm(after_in.astype(jnp.float32)).astype(jnp.bfloat16)
    projected = jnp.dot(normed_mix, trans_in_w, preferred_element_type=jnp.float32)
    half_width = trans_in_w.shape[1] // 2
    hidden = (jax.nn.silu(projected[..., :half_width]) * projected[..., half_width:]).astype(
        jnp.bfloat16
    )
    result = after_in.astype(jnp.float32) + jnp.dot(
        hidden, trans_out_w, preferred_element_type=jnp.float32
    )
    return result.astype(jnp.bfloat16)


def solution(mesh):
    in_specs = (
        P(("crop", "row"), "col", None),
        P(("crop", "row"), "col"),
        P(),
        P(),
        P(),
        P(),
        P(),
        P(),
        P(),
        P(),
        P(),
        P(),
    )
    out_specs = P(("crop", "row"), "col", None)
    return jax.shard_map(shards, mesh=mesh, in_specs=in_specs, out_specs=out_specs, check_vma=False)
```

profile of v0, /device:TPU:0, one launch (start us, length us, event | category | flops | bytes accessed | tf_op | source)
XLA Modules:
  0.0 162.0 jit_solution(13725264176336256992)
XLA Ops:
  6.5 1.2 convert_reduce_fusion
  7.8 1.3 fusion.17
  9.1 1.4 fusion.44
  10.6 1.3 fusion.46
  13.0 10.7 %all_to_all.46 = bf16[32,32,128]{2,1,0:T(8,128)(2,1)S(1)} all-to-all(bf16[32,32,128]{2,1,0:T(8,128)(2,1)S(1)} %get-tuple-element.8), channel_id=1, replica_groups=mesh['row'=4,'col'=4,'crop'=2] {'row'}, dimensions={0} | all-to-all | bytes 524288 | tf_op jit(solution)/shard_map/all_to_all | solution.py:49
  23.7 21.0 %all_to_all.47 = bf16[32,32,128]{2,1,0:T(8,128)(2,1)S(1)} all-to-all(bf16[32,32,128]{2,1,0:T(8,128)(2,1)S(1)} %all_to_all.46), channel_id=1, replica_groups=mesh['row'=4,'col'=4,'crop'=2] {'col'}, dimensions={0} | all-to-all | bytes 524288 | tf_op jit(solution)/shard_map/all_to_all | solution.py:48
  46.5 3.4 %all-gather.7.cloned.1.call-done = bf16[32,128,128]{2,1,0:T(8,128)(2,1)} async-done(((bf16[32,32,128]{2,1,0:T(8,128)(2,1)}), bf16[32,128,128]{2,1,0:T(8,128)(2,1)}) %all-gather.7.cloned.1.call-update) | async-done | bytes 1048592 | tf_op jit(solution)/shard_map/all_gather | solution.py:56
  49.9 2.7 %copy.67 = bf16[32,128,128]{1,0,2:T(8,128)(2,1)} copy(bf16[32,128,128]{2,1,0:T(8,128)(2,1)} %all-gather.7.cloned.1.call-done) | data formatting | bytes 2097152 | tf_op jit(solution)/shard_map/all_gather | solution.py:56
  52.5 24.4 %all-gather.5.cloned.1.call-done = bf16[32,128,128]{1,0,2:T(8,128)(2,1)} async-done(((bf16[8,128,128]{1,0,2:T(8,128)(2,1)}), bf16[32,128,128]{1,0,2:T(8,128)(2,1)}) %all-gather.5.cloned.1.call-update) | async-done | bytes 1048592 | tf_op jit(solution)/shard_map/all_gather | solution.py:60
  76.9 2.2 %bitcast_reduce_fusion.1 = (f32[32,32]{0,1:T(8,128)S(1)}, f32[128,32,32]{2,1,0:T(8,128)S(1)}) fusion(bf16[32,128,128]{1,0,2:T(8,128)(2,1)} %all-gather.5.cloned.1.call-done, bf16[32,128,128]{1,0,2:T(8,128)(2,1)} %copy.67), kind=kOutput, calls=%fused_computation.5 | convolution fusion | flops 33684480 | bytes 2625536 | tf_op jit(solution)/shard_map/ikh,jkh->ijh/dot_general | solution.py:57
  79.8 1.3 multiply_convert_fusion.1
  81.1 2.7 %copy.72 = bf16[32,32,128]{2,1,0:T(8,128)(2,1)S(1)} copy(bf16[32,32,128]{0,1,2:T(8,128)(2,1)} %multiply_convert_fusion.1) | data formatting | bytes 524288 | tf_op jit(solution)/shard_map/convert_element_type | solution.py:26
  85.5 1.0 fusion.20
  86.7 13.1 %all_to_all.48 = bf16[32,32,128]{2,0,1:T(8,128)(2,1)S(1)} all-to-all(bf16[32,32,128]{2,0,1:T(8,128)(2,1)S(1)} %copy.73), channel_id=1, replica_groups=mesh['row'=4,'col'=4,'crop'=2] {'col'}, dimensions={1} | all-to-all | bytes 524288 | tf_op jit(solution)/shard_map/all_to_all | solution.py:67
  99.8 8.2 %all_to_all.49 = bf16[32,32,128]{2,0,1:T(8,128)(2,1)S(1)} all-to-all(bf16[32,32,128]{2,0,1:T(8,128)(2,1)S(1)} %all_to_all.48), channel_id=1, replica_groups=mesh['row'=4,'col'=4,'crop'=2] {'row'}, dimensions={1} | all-to-all | bytes 524288 | tf_op jit(solution)/shard_map/all_to_all | solution.py:66
  109.1 1.1 fusion.3
  110.2 3.4 %all-gather.9.cloned.1.call-done = bf16[128,32,128]{2,1,0:T(8,128)(2,1)} async-done(((bf16[32,32,128]{2,1,0:T(8,128)(2,1)}), bf16[128,32,128]{2,1,0:T(8,128)(2,1)}) %all-gather.9.cloned.1.call-update) | async-done | bytes 1048592 | tf_op jit(solution)/shard_map/all_gather | solution.py:74
  113.6 3.2 %copy.77 = bf16[128,32,128]{0,1,2:T(8,128)(2,1)} copy(bf16[128,32,128]{2,1,0:T(8,128)(2,1)} %all-gather.9.cloned.1.call-done) | data formatting | bytes 2097152 | tf_op jit(solution)/shard_map/all_gather | solution.py:74
  116.8 27.7 %all-gather.11.cloned.1.call-done = bf16[128,32,128]{0,1,2:T(8,128)(2,1)} async-done(((bf16[128,8,128]{0,1,2:T(8,128)(2,1)}), bf16[128,32,128]{0,1,2:T(8,128)(2,1)}) %all-gather.11.cloned.1.call-update) | async-done | bytes 1048592 | tf_op jit(solution)/shard_map/all_gather | solution.py:77
  144.5 2.2 %bitcast_reduce_fusion = (f32[32,32]{0,1:T(8,128)S(1)}, f32[128,32,32]{2,1,0:T(8,128)S(1)}) fusion(bf16[128,32,128]{0,1,2:T(8,128)(2,1)} %copy.77, bf16[128,32,128]{0,1,2:T(8,128)(2,1)} %all-gather.11.cloned.1.call-done), kind=kOutput, calls=%fused_computation.3 | convolution fusion | flops 33684480 | bytes 2625536 | tf_op jit(solution)/shard_map/kih,kjh->ijh/dot_general | solution.py:75
  147.4 1.3 multiply_convert_fusion
  148.6 2.6 %copy.82 = bf16[32,32,128]{2,1,0:T(8,128)(2,1)S(1)} copy(bf16[32,32,128]{0,1,2:T(8,128)(2,1)} %multiply_convert_fusion) | data formatting | bytes 524288 | tf_op jit(solution)/shard_map/convert_element_type | solution.py:26
  151.3 1.4 fusion.61
  154.0 1.4 fusion.13
  (63 shorter events, 8.2 us)
Async XLA Ops:
  6.5 146.6 %copy-start = (bf16[128,1024]{1,0:T(8,128)(2,1)S(1)}, bf16[128,1024]{1,0:T(8,128)(2,1)}, u32[]{:S(2)}) copy-start(bf16[128,1024]{1,0:T(8,128)(2,1)} %param.22) | copy-start | bytes 786436
  6.5 4.0 %copy-start.1 = (bf16[32,32,128]{2,1,0:T(8,128)(2,1)S(1)}, bf16[32,32,128]{2,1,0:T(8,128)(2,1)}, u32[]{:S(2)}) copy-start(bf16[32,32,128]{2,1,0:T(8,128)(2,1)} %param.12) | copy-start | bytes 786436
  6.5 5.3 %copy-start.6 = (s32[32,32]{1,0:T(8,128)S(1)}, s32[32,32]{1,0:T(8,128)}, u32[]{:S(2)}) copy-start(s32[32,32]{1,0:T(8,128)} %param.13) | copy-start | bytes 12292
  6.5 43.3 %all-gather.7.cloned.1.call-start = ((), (), s32[]{:S(2)}) async-start(), calls=%async_computation.5 | async-start | bytes 1310720 | tf_op jit(solution)/shard_map/all_gather | solution.py:56
  11.9 33.8 %copy-start.8 = (bf16[128,128]{1,0:T(8,128)(2,1)S(1)}, bf16[128,128]{1,0:T(8,128)(2,1)}, u32[]{:S(2)}) copy-start(bf16[128,128]{1,0:T(8,128)(2,1)} %param.16) | copy-start | bytes 98308
  12.9 64.0 %all-gather.5.cloned.1.call-start = ((), (), s32[]{:S(2)}) async-start(), calls=%async_computation.4 | async-start | bytes 1310720 | tf_op jit(solution)/shard_map/all_gather | solution.py:60
  45.7 67.9 %all-gather.9.cloned.1.call-start = ((), (), s32[]{:S(2)}) async-start(), calls=%async_computation.6 | async-start | bytes 1310720 | tf_op jit(solution)/shard_map/all_gather | solution.py:74
  79.8 3.9 %copy-start.5 = (bf16[128,128]{1,0:T(8,128)(2,1)S(1)}, bf16[128,128]{1,0:T(8,128)(2,1)}, u32[]{:S(2)}) copy-start(bf16[128,128]{1,0:T(8,128)(2,1)} %param.17) | copy-start | bytes 98308
  81.1 3.8 %copy-start.2 = (bf16[128,256]{1,0:T(8,128)(2,1)S(1)}, bf16[128,256]{1,0:T(8,128)(2,1)}, u32[]{:S(2)}) copy-start(bf16[128,256]{1,0:T(8,128)(2,1)} %param.18) | copy-start | bytes 196612
  83.7 1.4 copy-start.3
  86.5 22.6 %copy-start.9 = (bf16[128,128]{1,0:T(8,128)(2,1)S(1)}, bf16[128,128]{1,0:T(8,128)(2,1)}, u32[]{:S(2)}) copy-start(bf16[128,128]{1,0:T(8,128)(2,1)} %param.20) | copy-start | bytes 98308
  86.5 58.0 %all-gather.11.cloned.1.call-start = ((), (), s32[]{:S(2)}) async-start(), calls=%async_computation.7 | async-start | bytes 1310720 | tf_op jit(solution)/shard_map/all_gather | solution.py:77
  147.4 3.9 %copy-start.4 = (bf16[128,128]{1,0:T(8,128)(2,1)S(1)}, bf16[128,128]{1,0:T(8,128)(2,1)}, u32[]{:S(2)}) copy-start(bf16[128,128]{1,0:T(8,128)(2,1)} %param.21) | copy-start | bytes 98308
  153.1 0.9 copy-start.7
Sparse Core Ops, SparseCore 0:
  13.1 36.7 all-gather.6
  51.7 25.2 all-gather.4
  86.6 26.9 all-gather.8
  115.0 29.4 all-gather.10
where the time goes:
time: 163 us; the launch traced here: 162 us
  waiting for transfers between devices  59 us (36%)
  blocking collectives  53.1 us (33%)
  local copies, waits for them, and re-layouts  14 us (9%)
  matrix products  13.4 us (8%)
  between operations  13.4 us (8%)
  other arithmetic  8.94 us (5%)
    all_gather x1, waiting for transfers between devices, shards(): lax.all_gather(turned_left, 'col', axis=1, tiled=True)  27.7 us
    all_gather x1, waiting for transfers between devices, shards(): lax.all_gather(turned_right, 'row', axis=0, tiled=True)  24.4 us
    all_to_all x1, blocking collectives, shards(): lax.all_to_all(lax.all_to_all(outbound, 'row', split_axis=0, concat_axis=...  21 us
    all_to_all x1, blocking collectives, shards(): lax.all_to_all(outbound_left, 'col', split_axis=1, concat_axis=1, tiled=T...  13.1 us
    all_to_all x1, blocking collectives, shards(): lax.all_to_all(outbound, 'row', split_axis=0, concat_axis=0, tiled=True)  10.7 us
    all_to_all x1, blocking collectives, shards(): lax.all_to_all(lax.all_to_all(outbound_left, 'col', split_axis=1, concat_...  8.25 us
    convert_element_type x2, local copies, waits for them, and re-layouts, finish(): tri_norm = layer_norm(triangle).astype(jnp.bfloat16)  5.27 us
    all_gather x1, waiting for transfers between devices, shards(): column_panel = lax.all_gather(right_tile, 'row', axis=0, tiled=True)  3.41 us
  transfers between devices with their start and end apart: 4, of which 4 were waited for; matrix products, arithmetic and copies ran while one was open for 6% of the time, Pallas kernels for 0%

commit v1 on v0

--- a/solution.py
+++ b/solution.py
@@ -4,6 +4,24 @@
 from jax.sharding import PartitionSpec as P
 
 epsilon = 1e-05
+
+
+def on_each_block(shard, axis, dim, apply, out_dim):
+    peers, position, rows = (lax.axis_size(axis), lax.axis_index(axis), shard.shape[dim])
+    ahead = [(i, (i + 1) % peers) for i in range(peers)]
+    held, out = (shard, None)
+    for step in range(peers):
+        source = (position - step) % peers
+        coming = lax.ppermute(held, axis, ahead) if step < peers - 1 else None
+        made = apply(held, source * rows)
+        length = made.shape[out_dim]
+        if out is None:
+            out = jnp.zeros(
+                (*made.shape[:out_dim], peers * length, *made.shape[out_dim + 1 :]), made.dtype
+            )
+        out = lax.dynamic_update_slice_in_dim(out, made, source * length, axis=out_dim)
+        held = coming
+    return out
 
 
 def layer_norm(values):
@@ -54,11 +72,14 @@
     )
     left_tile = gated(normed_out, out_left_w, mask_vals)
     gathered = lax.all_gather(left_tile, "col", axis=1, tiled=True)
-    triangle = jnp.einsum(
-        "ikh,jkh->ijh",
-        gathered,
-        lax.all_gather(turned_right, "row", axis=0, tiled=True),
-        preferred_element_type=jnp.float32,
+    triangle = on_each_block(
+        turned_right,
+        "row",
+        0,
+        lambda part, offset: jnp.einsum(
+            "ikh,jkh->ijh", gathered, part, preferred_element_type=jnp.float32
+        ),
+        1,
     )
     middle = finish(pair_repr, normed_out, triangle, out_gate_w, out_final_w)
     normed_in = layer_norm(middle.astype(jnp.float32)).astype(jnp.bfloat16)

time: 163 us -> 148 us (0.908)
  waiting for transfers between devices: 59 us -> 48.3 us
  local copies, waits for them, and re-layouts: 14 us -> 10.6 us
  blocking collectives: 53.1 us -> 50.7 us
  matrix products: 13.4 us -> 15.2 us
    all_gather x1 -> x0, waiting for transfers between devices: 24.4 us -> none  [shards(): lax.all_gather(turned_right, 'row', axis=0, tiled=True)]
    ppermute x0 -> x3, waiting for transfers between devices: none -> 16.1 us  [on_each_block(): coming = lax.ppermute(held, axis, ahead) if step < peers - 1 else None]
    all_gather x1, waiting for transfers between devices: 3.41 us -> 0.01 us  [shards(): gathered = lax.all_gather(left_tile, 'col', axis=1, tiled=True)]
    convert_element_type x2 -> x1, local copies, waits for them, and re-layouts: 5.27 us -> 2.62 us  [finish(): tri_norm = layer_norm(triangle).astype(jnp.bfloat16)]
    all_to_all x1, blocking collectives: 13.1 us -> 10.8 us  [shards(): lax.all_to_all(outbound_left, 'col', split_axis=1, concat_axis=1, tiled=T...]
    dot_general x1 -> x4, matrix products: 2.2 us -> 3.5 us  [shards(): jnp.einsum('ikh,jkh->ijh', gathered, part, preferred_element_type=jnp.flo...]
  transfers between devices with their start and end apart: 4 -> 6, of which waited for: 4 -> 5; matrix products, arithmetic and copies ran while one was open for 6% -> 7% of each run, Pallas kernels for 0% -> 0%
where the time goes in v1:
time: 148 us; the launch traced here: 147 us
  blocking collectives  50.7 us (34%)
  waiting for transfers between devices  48.3 us (33%)
  matrix products  15.2 us (10%)
  between operations  13.5 us (9%)
  local copies, waits for them, and re-layouts  10.6 us (7%)
  other arithmetic  7.93 us (5%)
    all_gather x1, waiting for transfers between devices, shards(): lax.all_gather(turned_left, 'col', axis=1, tiled=True)  28.3 us
    all_to_all x1, blocking collectives, shards(): lax.all_to_all(lax.all_to_all(outbound, 'row', split_axis=0, concat_axis=...  21 us
    ppermute x3, waiting for transfers between devices, on_each_block(): coming = lax.ppermute(held, axis, ahead) if step < peers - 1 else None  16.1 us
    all_to_all x1, blocking collectives, shards(): lax.all_to_all(outbound_left, 'col', split_axis=1, concat_axis=1, tiled=T...  10.8 us
    all_to_all x1, blocking collectives, shards(): lax.all_to_all(outbound, 'row', split_axis=0, concat_axis=0, tiled=True)  10.7 us
    all_to_all x1, blocking collectives, shards(): lax.all_to_all(lax.all_to_all(outbound_left, 'col', split_axis=1, concat_...  8.1 us
    all_gather x1, waiting for transfers between devices, shards(): column_panel = lax.all_gather(right_tile, 'row', axis=0, tiled=True)  3.85 us
    dot_general x4, matrix products, shards(): jnp.einsum('ikh,jkh->ijh', gathered, part, preferred_element_type=jnp.flo...  3.5 us
  transfers between devices with their start and end apart: 6, of which 5 were waited for; matrix products, arithmetic and copies ran while one was open for 7% of the time, Pallas kernels for 0%

profile of v1, /device:TPU:0, one launch (start us, length us, event | category | flops | bytes accessed | tf_op | source)
XLA Modules:
  0.0 147.3 jit_solution(13939790397222525213)
XLA Ops:
  6.5 1.2 convert_reduce_fusion
  7.8 1.3 fusion.17
  9.1 1.4 fusion.46
  10.6 1.3 fusion.48
  13.0 10.7 %all_to_all.46 = bf16[32,32,128]{2,1,0:T(8,128)(2,1)S(1)} all-to-all(bf16[32,32,128]{2,1,0:T(8,128)(2,1)S(1)} %get-tuple-element.8), channel_id=1, replica_groups=mesh['row'=4,'col'=4,'crop'=2] {'row'}, dimensions={0} | all-to-all | bytes 524288 | tf_op jit(solution)/shard_map/all_to_all | solution.py:67
  23.7 21.0 %all_to_all.47 = bf16[32,32,128]{2,1,0:T(8,128)(2,1)S(1)} all-to-all(bf16[32,32,128]{2,1,0:T(8,128)(2,1)S(1)} %all_to_all.46), channel_id=1, replica_groups=mesh['row'=4,'col'=4,'crop'=2] {'col'}, dimensions={0} | all-to-all | bytes 524288 | tf_op jit(solution)/shard_map/all_to_all | solution.py:66
  44.9 1.0 collective-permute-start
  45.9 6.3 %collective-permute-done = bf16[8,128,128]{1,0,2:T(8,128)(2,1)S(1)} collective-permute-done((bf16[8,128,128]{1,0,2:T(8,128)(2,1)S(1)}, bf16[8,128,128]{1,0,2:T(8,128)(2,1)S(1)}, u32[]{:S(2)}, u32[]{:S(2)}) %collective-permute-start) | collective-permute-done | bytes 262176 | tf_op jit(solution)/shard_map/ppermute | solution.py:15
  53.0 7.0 %collective-permute-done.1 = bf16[8,128,128]{1,0,2:T(8,128)(2,1)S(1)} collective-permute-done((bf16[8,128,128]{1,0,2:T(8,128)(2,1)S(1)}, bf16[8,128,128]{1,0,2:T(8,128)(2,1)S(1)}, u32[]{:S(2)}, u32[]{:S(2)}) %collective-permute-start.1) | collective-permute-done | bytes 262176 | tf_op jit(solution)/shard_map/ppermute | solution.py:15
  60.0 1.9 %copy.94 = bf16[32,128,128]{1,0,2:T(8,128)(2,1)S(1)} copy(bf16[32,128,128]{2,1,0:T(8,128)(2,1)} %all-gather.4.cloned.1.call-done) | data formatting | bytes 2097152 | tf_op jit(solution)/shard_map/all_gather | solution.py:74
  64.6 2.8 %collective-permute-done.2 = bf16[8,128,128]{1,0,2:T(8,128)(2,1)} collective-permute-done((bf16[8,128,128]{1,0,2:T(8,128)(2,1)S(1)}, bf16[8,128,128]{1,0,2:T(8,128)(2,1)}, u32[]{:S(2)}, u32[]{:S(2)}) %collective-permute-start.2) | collective-permute-done | bytes 262176 | tf_op jit(solution)/shard_map/ppermute | solution.py:15
  67.4 1.6 %convolution_bitcast_fusion = f32[32,8,128]{0,1,2:T(8,128)S(1)} fusion(bf16[8,128,128]{1,0,2:T(8,128)(2,1)} %collective-permute-done.2, bf16[32,128,128]{1,0,2:T(8,128)(2,1)S(1)} %copy.94), kind=kOutput, calls=%fused_computation.13 | convolution fusion | flops 8388608 | bytes 1441792 | tf_op jit(solution)/shard_map/ikh,jkh->ijh/dot_general | solution.py:79
  72.2 1.0 fusion.20
  73.4 10.8 %all_to_all.48 = bf16[32,32,128]{2,0,1:T(8,128)(2,1)S(1)} all-to-all(bf16[32,32,128]{2,0,1:T(8,128)(2,1)S(1)} %copy.103), channel_id=1, replica_groups=mesh['row'=4,'col'=4,'crop'=2] {'col'}, dimensions={1} | all-to-all | bytes 524288 | tf_op jit(solution)/shard_map/all_to_all | solution.py:88
  84.2 8.1 %all_to_all.49 = bf16[32,32,128]{2,0,1:T(8,128)(2,1)S(1)} all-to-all(bf16[32,32,128]{2,0,1:T(8,128)(2,1)S(1)} %all_to_all.48), channel_id=1, replica_groups=mesh['row'=4,'col'=4,'crop'=2] {'row'}, dimensions={1} | all-to-all | bytes 524288 | tf_op jit(solution)/shard_map/all_to_all | solution.py:87
  93.4 1.1 fusion.3
  94.5 3.8 %all-gather.6.cloned.1.call-done = bf16[128,32,128]{2,1,0:T(8,128)(2,1)} async-done(((bf16[32,32,128]{2,1,0:T(8,128)(2,1)}), bf16[128,32,128]{2,1,0:T(8,128)(2,1)}) %all-gather.6.cloned.1.call-update) | async-done | bytes 1048592 | tf_op jit(solution)/shard_map/all_gather | solution.py:95
  98.3 3.2 %copy.107 = bf16[128,32,128]{0,1,2:T(8,128)(2,1)} copy(bf16[128,32,128]{2,1,0:T(8,128)(2,1)} %all-gather.6.cloned.1.call-done) | data formatting | bytes 2097152 | tf_op jit(solution)/shard_map/all_gather | solution.py:95
  101.5 28.3 %all-gather.8.cloned.1.call-done = bf16[128,32,128]{0,1,2:T(8,128)(2,1)} async-done(((bf16[128,8,128]{0,1,2:T(8,128)(2,1)}), bf16[128,32,128]{0,1,2:T(8,128)(2,1)}) %all-gather.8.cloned.1.call-update) | async-done | bytes 1048592 | tf_op jit(solution)/shard_map/all_gather | solution.py:98
  129.9 2.2 %bitcast_reduce_fusion = (f32[32,32]{0,1:T(8,128)S(1)}, f32[128,32,32]{2,1,0:T(8,128)S(1)}) fusion(bf16[128,32,128]{0,1,2:T(8,128)(2,1)} %copy.107, bf16[128,32,128]{0,1,2:T(8,128)(2,1)} %all-gather.8.cloned.1.call-done), kind=kOutput, calls=%fused_computation.3 | convolution fusion | flops 33684480 | bytes 2625536 | tf_op jit(solution)/shard_map/kih,kjh->ijh/dot_general | solution.py:96
  132.8 1.3 multiply_convert_fusion
  134.0 2.6 %copy.112 = bf16[32,32,128]{2,1,0:T(8,128)(2,1)S(1)} copy(bf16[32,32,128]{0,1,2:T(8,128)(2,1)} %multiply_convert_fusion) | data formatting | bytes 524288 | tf_op jit(solution)/shard_map/convert_element_type | solution.py:44
  136.7 1.4 fusion.63
  139.4 1.4 fusion.13
  (73 shorter events, 11.0 us)
Async XLA Ops:
  6.5 131.9 %copy-start = (bf16[128,1024]{1,0:T(8,128)(2,1)S(1)}, bf16[128,1024]{1,0:T(8,128)(2,1)}, u32[]{:S(2)}) copy-start(bf16[128,1024]{1,0:T(8,128)(2,1)} %param.22) | copy-start | bytes 786436
  6.5 4.0 %copy-start.1 = (bf16[32,32,128]{2,1,0:T(8,128)(2,1)S(1)}, bf16[32,32,128]{2,1,0:T(8,128)(2,1)}, u32[]{:S(2)}) copy-start(bf16[32,32,128]{2,1,0:T(8,128)(2,1)} %param.12) | copy-start | bytes 786436
  6.5 5.3 %copy-start.6 = (s32[32,32]{1,0:T(8,128)S(1)}, s32[32,32]{1,0:T(8,128)}, u32[]{:S(2)}) copy-start(s32[32,32]{1,0:T(8,128)} %param.13) | copy-start | bytes 12292
  6.5 53.5 %all-gather.4.cloned.1.call-start = ((), (), s32[]{:S(2)}) async-start(), calls=%async_computation.4 | async-start | bytes 1310720 | tf_op jit(solution)/shard_map/all_gather | solution.py:74
  11.9 40.5 %copy-start.8 = (bf16[128,128]{1,0:T(8,128)(2,1)S(1)}, bf16[128,128]{1,0:T(8,128)(2,1)}, u32[]{:S(2)}) copy-start(bf16[128,128]{1,0:T(8,128)(2,1)} %param.16) | copy-start | bytes 98308
  12.9 85.4 %all-gather.6.cloned.1.call-start = ((), (), s32[]{:S(2)}) async-start(), calls=%async_computation.5 | async-start | bytes 1310720 | tf_op jit(solution)/shard_map/all_gather | solution.py:95
  44.9 7.3 %collective-permute-start = (bf16[8,128,128]{1,0,2:T(8,128)(2,1)S(1)}, bf16[8,128,128]{1,0,2:T(8,128)(2,1)S(1)}, u32[]{:S(2)}, u32[]{:S(2)}) collective-permute-start(bf16[8,128,128]{1,0,2:T(8,128)(2,1)S(1)} %copy.93), channel_id=1, source_target_pairs={{0,8},{8,16},{16,24},{24,0},{1,9},{9,17},{17,25},{25,1},{2,10},{10... | collective-permute-start | bytes 786440 | tf_op jit(solution)/shard_map/ppermute | solution.py:15
  52.2 7.8 %collective-permute-start.1 = (bf16[8,128,128]{1,0,2:T(8,128)(2,1)S(1)}, bf16[8,128,128]{1,0,2:T(8,128)(2,1)S(1)}, u32[]{:S(2)}, u32[]{:S(2)}) collective-permute-start(bf16[8,128,128]{1,0,2:T(8,128)(2,1)S(1)} %collective-permute-done), channel_id=1, source_target_pairs={{0,8},{8,16},{16,24},{24,0},{1,9},{9,17},{17,25},{25,1},{2,10},{10... | collective-permute-start | bytes 786440 | tf_op jit(solution)/shard_map/ppermute | solution.py:15
  60.0 7.4 %collective-permute-start.2 = (bf16[8,128,128]{1,0,2:T(8,128)(2,1)S(1)}, bf16[8,128,128]{1,0,2:T(8,128)(2,1)}, u32[]{:S(2)}, u32[]{:S(2)}) collective-permute-start(bf16[8,128,128]{1,0,2:T(8,128)(2,1)S(1)} %collective-permute-done.1), channel_id=1, source_target_pairs={{0,8},{8,16},{16,24},{24,0},{1,9},{9,17},{17,25},{25,1},{2,10},{10... | collective-permute-start | bytes 786440 | tf_op jit(solution)/shard_map/ppermute | solution.py:15
  69.0 1.0 copy-start.5
  69.6 2.0 %copy-start.2 = (bf16[128,256]{1,0:T(8,128)(2,1)S(1)}, bf16[128,256]{1,0:T(8,128)(2,1)}, u32[]{:S(2)}) copy-start(bf16[128,256]{1,0:T(8,128)(2,1)} %param.18) | copy-start | bytes 196612
  70.0 1.9 %copy-start.3 = (bf16[128,256]{1,0:T(8,128)(2,1)S(1)}, bf16[128,256]{1,0:T(8,128)(2,1)}, u32[]{:S(2)}) copy-start(bf16[128,256]{1,0:T(8,128)(2,1)} %param.19) | copy-start | bytes 196612
  73.2 20.2 %copy-start.9 = (bf16[128,128]{1,0:T(8,128)(2,1)S(1)}, bf16[128,128]{1,0:T(8,128)(2,1)}, u32[]{:S(2)}) copy-start(bf16[128,128]{1,0:T(8,128)(2,1)} %param.20) | copy-start | bytes 98308
  73.2 56.6 %all-gather.8.cloned.1.call-start = ((), (), s32[]{:S(2)}) async-start(), calls=%async_computation.6 | async-start | bytes 1310720 | tf_op jit(solution)/shard_map/all_gather | solution.py:98
  132.8 3.9 %copy-start.4 = (bf16[128,128]{1,0:T(8,128)(2,1)S(1)}, bf16[128,128]{1,0:T(8,128)(2,1)}, u32[]{:S(2)}) copy-start(bf16[128,128]{1,0:T(8,128)(2,1)} %param.21) | copy-start | bytes 98308
  138.5 0.9 copy-start.7
Sparse Core Ops, SparseCore 0:
  13.1 36.7 all-gather.3
  73.4 24.9 all-gather.5
  99.9 29.9 all-gather.7
